TPU v7x, 256 devices: a whole 4x4x8 slice. The times are simulated.
256 devices in a mesh: depth: 8 (over z), col: 4 (over y), row: 8 (over x, core).
Axes of the slice: x: 4, y: 4, z: 8, core: 2. Of those that a mesh axis runs over, the one named last changes fastest.
Arguments:
- weight: bfloat16 [16384, 16384], P(('row', 'depth'), 'col')
- rhs_stack: bfloat16 [3, 16384, 4096], P(None, ('row', 'depth'), 'col')
Outputs:
- output: bfloat16 [3, 16384, 4096], P(None, ('row', 'depth'), 'col')
All inputs are finite; a program needn't handle non-finite values.
Results may differ from a plain program's by a relative error of at most 0.001.
Values are sent between devices in bfloat16 or wider.
A program may use at most 768 MiB of HBM per device.

v0:
```python
import jax
import jax.numpy as jnp
from jax import lax
from jax.sharding import PartitionSpec as P

ALL_AXES = ("depth", "col", "row")


def solution(mesh):
    depth_size = mesh.shape["depth"]
    col_size = mesh.shape["col"]
    row_size = mesh.shape["row"]
    group_size = row_size // col_size
    layer_steps = row_size // depth_size
    all_coords = [(layer_idx, col_idx, row_idx) for layer_idx in range(depth_size) for col_idx in range(col_size) for row_idx in range(row_size)]

    def linear_index(coords):
        layer_idx, col_idx, row_idx = coords
        return (layer_idx * col_size + col_idx) * row_size + row_idx

    def a_source(coords, extra):
        layer_idx, col_idx, row_idx = coords
        block_shift = (row_idx + layer_idx * layer_steps) // group_size
        return linear_index((layer_idx, (col_idx + block_shift + extra) % col_size, row_idx))

    def x_source(coords, piece_idx):
        layer_idx, col_idx, row_idx = coords
        src_row = (row_idx + col_idx * group_size + piece_idx + layer_idx * layer_steps) % row_size
        return linear_index((layer_idx, col_idx, src_row))

    perm_a_near = [(a_source(coords, 0), linear_index(coords)) for coords in all_coords]
    perm_a_next = [(a_source(coords, 1), linear_index(coords)) for coords in all_coords]
    perm_x_pieces = [[(x_source(coords, piece_idx), linear_index(coords)) for coords in all_coords] for piece_idx in range(group_size)]
    perm_col_shift = [(col_idx, (col_idx - 1) % col_size) for col_idx in range(col_size)]
    perm_row_shift = [(row_idx, (row_idx - 1) % row_size) for row_idx in range(row_size)]

    def local_product(w_local, x_local):
        rhs_count = x_local.shape[0]
        slice_rows = x_local.shape[1]
        block_cols = x_local.shape[2] // group_size
        w_layer = lax.all_gather(w_local, "depth", axis=0, tiled=True)
        block_rows = w_layer.shape[0]
        x_split = jnp.transpose(x_local.reshape(rhs_count, slice_rows, group_size, block_cols), (2, 1, 0, 3))
        x_layer = lax.all_gather(x_split, "depth", axis=1, tiled=True)
        layer_idx = lax.axis_index("depth")
        row_idx = lax.axis_index("row")
        offset = (row_idx + layer_idx * layer_steps) % group_size
        w_near = lax.ppermute(w_layer, ALL_AXES, perm_a_near)
        if group_size > 1:
            w_next = lax.ppermute(w_layer, ALL_AXES, perm_a_next)
            w_pair = jnp.concatenate([w_near, w_next], axis=1).reshape(block_rows, 2 * group_size, block_rows)
            w_start = lax.dynamic_slice_in_dim(w_pair, offset, group_size, axis=1)
        else:
            w_start = w_near.reshape(block_rows, 1, block_rows)
        w_blocks = jnp.transpose(w_start, (1, 0, 2))
        x_blocks = jnp.stack([lax.ppermute(x_layer[piece_idx], ALL_AXES, perm_x_pieces[piece_idx]) for piece_idx in range(group_size)], axis=0)
        partial_sum = jnp.einsum("tik,tkrm->tirm", w_blocks, x_blocks, preferred_element_type=jnp.float32)
        for step_idx in range(1, layer_steps):
            w_recv = lax.ppermute(w_blocks[0], "col", perm_col_shift)
            w_blocks = jnp.concatenate([w_blocks[1:], w_recv[None]], axis=0)
            x_blocks = lax.ppermute(x_blocks, "row", perm_row_shift)
            partial_sum = partial_sum + jnp.einsum("tik,tkrm->tirm", w_blocks, x_blocks, preferred_element_type=jnp.float32)
        reduced = lax.psum_scatter(partial_sum, "depth", scatter_dimension=1, tiled=True)
        rounded = reduced.astype(jnp.bfloat16)
        return jnp.transpose(rounded, (2, 1, 0, 3)).reshape(rhs_count, slice_rows, group_size * block_cols)

    return jax.shard_map(local_product, mesh=mesh, in_specs=(P(("row", "depth"), "col"), P(None, ("row", "depth"), "col")), out_specs=P(None, ("row", "depth"), "col"), check_vma=False)
```

profile of v0, /device:TPU:2, one launch (start us, length us, event | category | flops | bytes accessed | tf_op | source)
XLA Modules:
  0.0 1269.2 jit_solution(10930858735108607839)
XLA Ops:
  6.5 0.0 all-gather.3.cloned.1.call-start
  6.5 4.1 copy.3
  10.6 0.0 all-gather.3.cloned.1.call-update
  10.6 0.0 all-gather.5.cloned.1.call-start
  10.7 1.7 copy.5
  12.4 1.6 copy.6
  14.0 0.0 all-gather.5.cloned.1.call-update
  14.0 0.0 reduce-scatter.2.cloned.1.call-start
  14.0 176.6 %all-gather.3.cloned.1.call-done = bf16[2048,4096]{0,1:T(8,128)(2,1)} async-done(((bf16[256,4096]{0,1:T(8,128)(2,1)}), bf16[2048,4096]{0,1:T(8,128)(2,1)}) %all-gather.3.cloned.1.call-update) | async-done | bytes 16777232 | tf_op jit(solution)/shard_map/all_gather | solution.py:41
  190.7 4.9 collective-permute-start.1
  195.6 3.1 collective-permute-start
  198.6 125.2 %all-gather.5.cloned.1.call-done = bf16[2,2048,3,512]{3,1,2,0:T(8,128)(2,1)} async-done(((bf16[2,256,3,512]{3,1,2,0:T(8,128)(2,1)}), bf16[2,2048,3,512]{3,1,2,0:T(8,128)(2,1)}) %all-gather.5.cloned.1.call-update) | async-done | bytes 12582928 | tf_op jit(solution)/shard_map/all_gather | solution.py:44
  323.8 10.1 slice_bitcast_fusion.1
  334.0 1.9 collective-permute-start.3
  335.9 48.4 %collective-permute-start.2 = (bf16[2048,3,512]{2,0,1:T(8,128)(2,1)}, bf16[2048,3,512]{2,0,1:T(8,128)(2,1)}, u32[]{:S(2)}, u32[]{:S(2)}) collective-permute-start(bf16[2048,3,512]{2,0,1:T(8,128)(2,1)} %get-tuple-element.5), channel_id=1, source_target_pairs={{0,0},{1,1},{2,2},{3,3},{4,4},{5,5},{6,6},{7,7},{10,8},{11,9},{12,... | collective-permute-start | bytes 18874376 | tf_op jit(solution)/shard_map/ppermute | solution.py:56
  384.3 169.3 %collective-permute-done.1 = bf16[2048,4096]{0,1:T(8,128)(2,1)} collective-permute-done((bf16[2048,4096]{0,1:T(8,128)(2,1)}, bf16[2048,4096]{0,1:T(8,128)(2,1)}, u32[]{:S(2)}, u32[]{:S(2)}) %collective-permute-start.1) | collective-permute-done | bytes 16777248 | tf_op jit(solution)/shard_map/ppermute | solution.py:50
  553.6 360.7 %collective-permute-done = bf16[2048,4096]{0,1:T(8,128)(2,1)} collective-permute-done((bf16[2048,4096]{0,1:T(8,128)(2,1)}, bf16[2048,4096]{0,1:T(8,128)(2,1)}, u32[]{:S(2)}, u32[]{:S(2)}) %collective-permute-start) | collective-permute-done | bytes 16777248 | tf_op jit(solution)/shard_map/ppermute | solution.py:48
  914.4 23.8 %pad_maximum_fusion = bf16[2048,8192]{0,1:T(8,128)(2,1)} fusion(bf16[2048,4096]{0,1:T(8,128)(2,1)} %collective-permute-done.1, bf16[2048,4096]{0,1:T(8,128)(2,1)} %collective-permute-done), kind=kLoop, calls=%fused_computation | loop fusion | flops 67108864 | bytes 67108864 | tf_op jit(solution)/shard_map/concatenate | solution.py:51
  938.2 14.1 %constant_dynamic-slice_fusion = bf16[2048,2,2048]{0,2,1:T(8,128)(2,1)} fusion(bf16[2048,4,2048]{0,2,1:T(8,128)(2,1)} %bitcast.19, s32[]{:T(128)S(6)} %select_n.11), kind=kLoop, calls=%fused_computation.9 | loop fusion | bytes 33554436 | tf_op jit(solution)/shard_map/dynamic_slice | solution.py:52
  952.3 22.5 %copy.10 = bf16[2048,2,2048]{2,0,1:T(8,128)(2,1)} copy(bf16[2048,2,2048]{0,2,1:T(8,128)(2,1)} %constant_dynamic-slice_fusion) | data formatting | bytes 33554432
  974.8 0.0 collective-permute-done.3
  974.8 0.0 collective-permute-done.2
  974.8 35.1 %fusion = f32[2,2048,3,512]{3,1,2,0:T(8,128)} fusion(bf16[2048,2,2048]{2,0,1:T(8,128)(2,1)} %copy.10, bf16[1,2048,3,512]{3,1,2,0:T(8,128)(2,1)} %bitcast.9, bf16[1,2048,3,512]{3,1,2,0:T(8,128)(2,1)} %bitcast.7), kind=kOutput, calls=%fused_computation.1 | convolution fusion | flops 25794969600 | bytes 54525952 | tf_op jit(solution)/shard_map/tik,tkrm->tirm/dot_general | solution.py:57
  1010.0 0.0 reduce-scatter.2.cloned.1.call-update
  1010.0 248.1 %reduce-scatter.2.cloned.1.call-done = f32[2,256,3,512]{3,1,2,0:T(8,128)} async-done(((f32[2,2048,3,512]{3,1,2,0:T(8,128)}), f32[2,256,3,512]{3,1,2,0:T(8,128)}) %reduce-scatter.2.cloned.1.call-update) | async-done | bytes 3145744 | tf_op jit(solution)/shard_map/reduce_scatter | solution.py:63
  1258.1 2.1 convert_bitcast_fusion
  1260.2 0.7 copy.7
  1260.9 1.7 copy.8
Async XLA Ops:
  6.5 184.1 %all-gather.3.cloned.1.call-start = ((), (), s32[]{:S(2)}) async-start(), calls=%async_computation.1 | async-start | bytes 18874368 | tf_op jit(solution)/shard_map/all_gather | solution.py:41
  10.6 313.2 %all-gather.5.cloned.1.call-start = ((), (), s32[]{:S(2)}) async-start(), calls=%async_computation.2 | async-start | bytes 14155776 | tf_op jit(solution)/shard_map/all_gather | solution.py:44
  14.0 1244.2 %reduce-scatter.2.cloned.1.call-start = ((), (), s32[]{:S(2)}) async-start(), calls=%async_computation.3 | async-start | bytes 28311552 | tf_op jit(solution)/shard_map/reduce_scatter | solution.py:63
  190.7 363.0 %collective-permute-start.1 = (bf16[2048,4096]{0,1:T(8,128)(2,1)}, bf16[2048,4096]{0,1:T(8,128)(2,1)}, u32[]{:S(2)}, u32[]{:S(2)}) collective-permute-start(bf16[2048,4096]{0,1:T(8,128)(2,1)} %all-gather.3.cloned.1.call-done), channel_id=1, source_target_pairs={{8,0},{9,1},{18,2},{19,3},{28,4},{29,5},{6,6},{7,7},{16,8},{17,9},... | collective-permute-start | bytes 50331656 | tf_op jit(solution)/shard_map/ppermute | solution.py:50
  195.6 718.8 %collective-permute-start = (bf16[2048,4096]{0,1:T(8,128)(2,1)}, bf16[2048,4096]{0,1:T(8,128)(2,1)}, u32[]{:S(2)}, u32[]{:S(2)}) collective-permute-start(bf16[2048,4096]{0,1:T(8,128)(2,1)} %all-gather.3.cloned.1.call-done), channel_id=1, source_target_pairs={{0,0},{1,1},{10,2},{11,3},{20,4},{21,5},{30,6},{31,7},{8,8},{9,9},... | collective-permute-start | bytes 50331656 | tf_op jit(solution)/shard_map/ppermute | solution.py:48
  334.0 640.9 %collective-permute-start.3 = (bf16[2048,3,512]{2,0,1:T(8,128)(2,1)}, bf16[2048,3,512]{2,0,1:T(8,128)(2,1)}, u32[]{:S(2)}, u32[]{:S(2)}) collective-permute-start(bf16[2048,3,512]{2,0,1:T(8,128)(2,1)} %get-tuple-element.6), channel_id=1, source_target_pairs={{1,0},{2,1},{3,2},{4,3},{5,4},{6,5},{7,6},{0,7},{11,8},{12,9},{13,... | collective-permute-start | bytes 18874376 | tf_op jit(solution)/shard_map/ppermute | solution.py:56
  335.9 639.0 %collective-permute-start.2 = (bf16[2048,3,512]{2,0,1:T(8,128)(2,1)}, bf16[2048,3,512]{2,0,1:T(8,128)(2,1)}, u32[]{:S(2)}, u32[]{:S(2)}) collective-permute-start(bf16[2048,3,512]{2,0,1:T(8,128)(2,1)} %get-tuple-element.5), channel_id=1, source_target_pairs={{0,0},{1,1},{2,2},{3,3},{4,4},{5,5},{6,6},{7,7},{10,8},{11,9},{12,... | collective-permute-start | bytes 18874376 | tf_op jit(solution)/shard_map/ppermute | solution.py:56
Sparse Core Ops, SparseCore 0:
  10.7 179.8 all-gather.2
  192.5 131.3 all-gather.4
  1010.1 247.9 reduce-scatter.1
where the time goes:
time: 1280 us; the launch traced here: 1270 us
  waiting for transfers between devices  1080 us (84%)
  starting transfers between devices  58.4 us (5%)
  local copies, waits for them, and re-layouts  56.5 us (4%)
  matrix products  35.1 us (3%)
  other arithmetic  25.9 us (2%)
  between operations  13.2 us (1%)
    ppermute x1, waiting for transfers between devices, local_product(): w_near = lax.ppermute(w_layer, ALL_AXES, perm_a_near)  361 us
    reduce_scatter x1, waiting for transfers between devices, local_product(): lax.psum_scatter(partial_sum, 'depth', scatter_dimension=1, tiled=True)  248 us
    all_gather x1, waiting for transfers between devices, local_product(): w_layer = lax.all_gather(w_local, 'depth', axis=0, tiled=True)  177 us
    ppermute x1, waiting for transfers between devices, local_product(): w_next = lax.ppermute(w_layer, ALL_AXES, perm_a_next)  169 us
    all_gather x1, waiting for transfers between devices, local_product(): x_layer = lax.all_gather(x_split, 'depth', axis=1, tiled=True)  125 us
    ppermute x2, starting transfers between devices, local_product(): lax.ppermute(x_layer[piece_idx], ALL_AXES, perm_x_pieces[piece_idx])  50.4 us
    dot_general x1, matrix products, local_product(): jnp.einsum('tik,tkrm->tirm', w_blocks, x_blocks, preferred_element_type=j...  35.1 us
    unnamed x3, local copies, waits for them, and re-layouts  28.3 us
  transfers between devices with their start and end apart: 7, of which 5 were waited for; matrix products, arithmetic and copies ran while one was open for 6% of the time, Pallas kernels for 0%

commit v1 on v0

v1 whole, which is shorter than its diff:
```python
import heapq

import jax
import jax.numpy as jnp
from jax import lax
from jax.experimental import pallas as pl
from jax.experimental.pallas import tpu as pltpu
from jax.sharding import PartitionSpec as P

MESH = pl.DeviceIdType.MESH
XS = 4
YS = 4
RHS = 3

A_UNIT_US = 11.3
X_UNIT_US = 8.5
A2A_UNIT_US = 2.9
D2D_UNIT_US = 4.0
HOP_US = 3.0
BLOCK_US = 9.0
PART_US = 2.6


def a_sends(unit):
    dx, dy, half, piece = unit
    major, minor = (dx, dy) if half == 0 else (dy, dx)
    fwd, back = ("x+", "x-") if half == 0 else ("y+", "y-")
    fwd2, back2 = ("y+", "y-") if half == 0 else ("x+", "x-")

    def named(new_major, new_minor):
        return (new_major, new_minor, half, piece) if half == 0 else (new_minor, new_major, half, piece)

    out = []
    if minor == 0:
        if major == 0:
            out += [(fwd, named(1, 0)), (back, named(3, 0))]
        elif major == 1 and piece == 0:
            out += [(fwd, named(2, 0))]
        elif major == 3 and piece == 1:
            out += [(back, named(2, 0))]
        out += [(fwd2, named(major, 1)), (back2, named(major, 3))]
    elif minor == 1 and piece == 0:
        out += [(fwd2, named(major, 2))]
    elif minor == 3 and piece == 1:
        out += [(back2, named(major, 2))]
    return out


def x_sends(unit, depth_size):
    dx, dz = unit
    mid = depth_size // 2
    out = []
    if dz < mid and (dz + 1 < mid or dx in (0, 1)):
        out.append(("z+", (dx, dz + 1)))
    back = (depth_size - dz) % depth_size
    if (dz == 0 or dz > mid) and (back + 1 < mid or dx not in (0, 1)):
        out.append(("z-", (dx, (dz - 1) % depth_size)))
    return out


def plan(depth_size):
    steps = []
    link_free = {}
    heap = []
    count = 0

    def send(link, name, now, cost):
        nonlocal count
        begin = max(now, link_free.get(link, 0.0))
        link_free[link] = begin + cost
        heapq.heappush(heap, (begin + cost + HOP_US, count, name))
        count += 1

    def handle(name, now):
        kind, unit = name
        steps.append(("have", name))
        if kind == "A":
            for link, there in a_sends(unit):
                send(link, ("A", there), now, A_UNIT_US)
        elif kind == "X":
            for link, there in x_sends(unit, depth_size):
                send(link, ("X", there), now, X_UNIT_US)

    for dx, link in ((1, "x+"), (3, "x-"), (2, "x+")):
        send(link, ("X", (dx, 0)), 0.0, 3 * A2A_UNIT_US)
    handle(("X", (0, 0)), 0.0)
    for half, piece in ((0, 0), (1, 0), (0, 1), (1, 1)):
        handle(("A", (0, 0, half, piece)), 0.0)

    done = set([("X", (0, 0))]) | set(("A", (0, 0, h, p)) for h in range(2) for p in range(2))
    x_all = set(("X", (dx, dz)) for dx in range(XS) for dz in range(depth_size))
    shared = set()

    def a_need(dxs, dy):
        return set(("A", (dx, dy, h, p)) for dx in dxs for h in range(2) for p in range(2))

    blocks = [(("mm", dy, None), a_need(range(XS), dy), BLOCK_US) for dy in (0, 1, 3)]
    blocks += [(("mm", 2, dx), a_need((dx,), 2), PART_US) for dx in (2, 1, 3, 0)]
    now = 0.0
    have_peer = False
    while heap or blocks:
        while heap and heap[0][0] <= now:
            _, _, name = heapq.heappop(heap)
            done.add(name)
            handle(name, now)
        for dz in range(depth_size):
            if dz not in shared and all(("X", (dx, dz)) in done for dx in range(XS)):
                shared.add(dz)
                steps.append(("share", dz))
                peer_at = now + D2D_UNIT_US + HOP_US
        ready = None
        if x_all <= done and now >= peer_at:
            if not have_peer:
                have_peer = True
                steps.append(("peer",))
            early = [b for b in blocks if b[0][2] is None]
            for block in (early or blocks):
                if block[1] <= done:
                    ready = block
                    break
        if ready is not None:
            blocks.remove(ready)
            steps.append(ready[0])
            now += ready[2]
        elif heap:
            now = max(now, heap[0][0])
        else:
            now = max(now, peer_at)
    return steps, now


def solution(mesh):
    depth_size = mesh.shape["depth"]
    steps, _ = plan(depth_size)

    def kernel(w_ref, x_ref, o_ref, a_all, x_all, acc, y_buf,
               a_ssem, a_rsem, x_ssem, x_rsem, d_ssem, d_rsem, t_ssem, t_rsem, y_ssem, y_rsem, l_sem):
        layer = lax.axis_index("depth")
        col = lax.axis_index("col")
        row = lax.axis_index("row")
        core = lax.rem(row, 2)
        xpos = row // 2
        rows, kcols = w_ref.shape
        unit = rows // 4
        sub = x_ref.shape[2] // XS

        def mod(value, size):
            return lax.rem(value + size, size)

        def row_peer(hops):
            return {"row": lax.rem(row + 2 * hops, 2 * XS)}

        sibling = {"row": row + 1 - 2 * core}
        links = {
            "x+": row_peer(1),
            "x-": row_peer(3),
            "y+": {"col": lax.rem(col + 1, YS)},
            "y-": {"col": lax.rem(col + YS - 1, YS)},
            "z+": {"depth": lax.rem(layer + 1, depth_size)},
            "z-": {"depth": lax.rem(layer + depth_size - 1, depth_size)},
        }

        barrier = pltpu.get_barrier_semaphore()
        partners = list(links.values()) + [row_peer(2), sibling]
        for partner in partners:
            pl.semaphore_signal(barrier, inc=1, device_id=partner, device_id_type=MESH)
        pl.semaphore_wait(barrier, len(partners))

        sent = []

        def a_index(name):
            dx, dy, half, piece = name
            return ((dx * 4 + dy) * 2 + half) * 2 + piece

        def a_slot(name):
            dx, dy, half, piece = name
            start = mod(xpos - dx, XS) * rows + (half * 2 + piece) * unit
            return a_all.at[mod(col - dy, YS), pl.ds(pl.multiple_of(start, unit), unit), :]

        def x_index(name):
            return name[1] * 4 + name[0]

        def x_rows(core_idx, dz):
            start = (core_idx * depth_size + mod(layer - dz, depth_size)) * rows
            return pl.ds(pl.multiple_of(start, rows), rows)

        def x_slot(name):
            return x_all.at[mod(xpos - name[0], XS), x_rows(core, name[1]), :]

        def remote(src, dst, ssem, rsem, device):
            copy = pltpu.make_async_remote_copy(src_ref=src, dst_ref=dst, send_sem=ssem, recv_sem=rsem, device_id=device, device_id_type=MESH)
            copy.start()
            sent.append(copy)

        def landed(slot, rsem):
            pltpu.make_async_remote_copy(src_ref=slot, dst_ref=slot, send_sem=l_sem.at[0], recv_sem=rsem, device_id=sibling, device_id_type=MESH).wait_recv()

        def x_part(hops, r):
            start = mod(xpos + hops, XS) * sub
            return x_ref.at[r, :, pl.ds(pl.multiple_of(start, sub), sub)]

        def x_dest(dx, r):
            return x_all.at[mod(xpos - dx, XS), x_rows(core, 0), pl.ds(r * sub, sub)]

        own_x = [pltpu.make_async_copy(x_part(0, r), x_dest(0, r), l_sem.at[1 + r]) for r in range(RHS)]
        for copy in own_x:
            copy.start()
        for hops in (1, 3, 2):
            for r in range(RHS):
                sem = hops * RHS + r
                remote(x_part(hops, r), x_dest(0, r), t_ssem.at[sem], t_rsem.at[sem], row_peer(hops))
        own_a = pltpu.make_async_copy(w_ref, a_all.at[col, pl.ds(pl.multiple_of(xpos * rows, rows), rows), :], l_sem.at[1 + RHS])
        own_a.start()
        acc[...] = jnp.zeros_like(acc)

        def matmul(dy, dx):
            chunk = mod(col - dy, YS)
            if dx is None:
                row0, nrows = 0, XS * rows
            else:
                row0, nrows = pl.multiple_of(mod(xpos - dx, XS) * rows, rows), rows
            kstep = min(1024, kcols)

            def body(idx, carry):
                r = idx // (kcols // kstep)
                k0 = pl.multiple_of(lax.rem(idx, kcols // kstep) * kstep, kstep)
                n0 = pl.multiple_of(r * sub, sub)
                lhs = a_all[chunk, pl.ds(row0, nrows), pl.ds(k0, kstep)]
                rhs = x_all[chunk, pl.ds(k0, kstep), pl.ds(n0, sub)]
                acc[pl.ds(row0, nrows), pl.ds(n0, sub)] += jnp.dot(lhs, rhs, preferred_element_type=jnp.float32)
                return carry

            lax.fori_loop(0, RHS * (kcols // kstep), body, 0)

        local = []

        def finish(dx):
            row0 = pl.multiple_of(mod(xpos - dx, XS) * rows, rows)
            for r in range(RHS):
                y_buf[dx, r] = acc[pl.ds(row0, rows), pl.ds(r * sub, sub)].astype(y_buf.dtype)
            dst = o_ref.at[:, :, pl.ds(pl.multiple_of(xpos * sub, sub), sub)]
            if dx == 0:
                copy = pltpu.make_async_copy(y_buf.at[0], dst, l_sem.at[2 + RHS])
                copy.start()
                local.append(copy)
            else:
                remote(y_buf.at[dx], dst, y_ssem.at[dx], y_rsem.at[dx], row_peer(XS - dx))

        own_waited = False
        for step in steps:
            if step[0] == "have":
                kind, name = step[1]
                if kind == "A":
                    if name[:2] != (0, 0):
                        landed(a_slot(name), a_rsem.at[a_index(name)])
                    for link, there in a_sends(name):
                        if name[:2] == (0, 0):
                            src = w_ref.at[pl.ds((name[2] * 2 + name[3]) * unit, unit), :]
                        else:
                            src = a_slot(name)
                        idx = a_index(there)
                        remote(src, a_slot(name), a_ssem.at[idx], a_rsem.at[idx], links[link])
                else:
                    if name == (0, 0):
                        for copy in own_x:
                            copy.wait()
                    elif name[1] == 0:
                        for r in range(RHS):
                            landed(x_dest(name[0], r), t_rsem.at[name[0] * RHS + r])
                    else:
                        landed(x_slot(name), x_rsem.at[x_index(name)])
                    for link, there in x_sends(name, depth_size):
                        idx = x_index(there)
                        remote(x_slot(name), x_slot(name), x_ssem.at[idx], x_rsem.at[idx], links[link])
            elif step[0] == "share":
                slot = x_all.at[:, x_rows(core, step[1]), :]
                remote(slot, slot, d_ssem.at[step[1]], d_rsem.at[step[1]], sibling)
            elif step[0] == "peer":
                for dz in range(depth_size):
                    landed(x_all.at[:, x_rows(1 - core, dz), :], d_rsem.at[dz])
            else:
                if not own_waited:
                    own_waited = True
                    own_a.wait()
                matmul(step[1], step[2])
                if step[2] is not None:
                    finish(step[2])

        for dx in range(1, XS):
            slot = o_ref.at[:, :, pl.ds(pl.multiple_of(mod(xpos + dx, XS) * sub, sub), sub)]
            landed(slot, y_rsem.at[dx])
        for copy in local:
            copy.wait()
        for copy in sent:
            copy.wait_send()

    def local_product(w_local, x_local):
        rows, kcols = w_local.shape
        sub = x_local.shape[2] // XS
        dma = pltpu.SemaphoreType.DMA
        return pl.pallas_call(
            kernel,
            out_shape=jax.ShapeDtypeStruct(x_local.shape, jnp.bfloat16),
            in_specs=[pl.BlockSpec(memory_space=pl.ANY)] * 2,
            out_specs=pl.BlockSpec(memory_space=pl.ANY),
            scratch_shapes=[
                pltpu.VMEM((YS, XS * rows, kcols), jnp.bfloat16),
                pltpu.VMEM((XS, kcols, RHS * sub), jnp.bfloat16),
                pltpu.VMEM((XS * rows, RHS * sub), jnp.float32),
                pltpu.VMEM((XS, RHS, rows, sub), jnp.bfloat16),
                dma((64,)), dma((64,)),
                dma((4 * depth_size,)), dma((4 * depth_size,)),
                dma((depth_size,)), dma((depth_size,)),
                dma((XS * RHS,)), dma((XS * RHS,)),
                dma((XS,)), dma((XS,)),
                dma((8,)),
            ],
            compiler_params=pltpu.CompilerParams(collective_id=0, has_side_effects=True, vmem_limit_bytes=67043328),
            cost_estimate=pl.CostEstimate(flops=2 * XS * rows * YS * kcols * RHS * sub, bytes_accessed=0, transcendentals=0),
            name="gather_matmul",
        )(w_local, x_local)

    return jax.shard_map(local_product, mesh=mesh, in_specs=(P(("row", "depth"), "col"), P(None, ("row", "depth"), "col")), out_specs=P(None, ("row", "depth"), "col"), check_vma=False)
```

time: 1280 us -> 223 us (0.17)
  waiting for transfers between devices: 1080 us -> 0 us
  Pallas kernels: 0 us -> 218 us
  starting transfers between devices: 58.4 us -> 0 us
  local copies, waits for them, and re-layouts: 56.5 us -> 2.67 us
  matrix products: 35.1 us -> 0 us
  other arithmetic: 25.9 us -> 0 us
  between operations: 13.2 us -> 0.01 us
    ppermute x4 -> x0, waiting for transfers between devices: 530 us -> none  [the longest x1 361 us: local_product(): w_near = lax.ppermute(w_layer, ALL_AXES, perm_a_near)]
    all_gather x2 -> x0, waiting for transfers between devices: 302 us -> none  [the longest x1 177 us: local_product(): w_layer = lax.all_gather(w_local, 'depth', axis=0, tiled=True)]
    reduce_scatter x1 -> x0, waiting for transfers between devices: 248 us -> none  [local_product(): lax.psum_scatter(partial_sum, 'depth', scatter_dimension=1, tiled=True)]
    pallas_call x0 -> x1, Pallas kernels: none -> 218 us  [local_product(): pl.pallas_call(kernel, out_shape=jax.ShapeDtypeStruct(x_local.shape, jnp....]
    ppermute x4 -> x0, starting transfers between devices: 58.3 us -> none  [the longest x2 50.4 us: local_product(): lax.ppermute(x_layer[piece_idx], ALL_AXES, perm_x_pieces[piece_idx])]
    dot_general x1 -> x0, matrix products: 35.1 us -> none  [local_product(): jnp.einsum('tik,tkrm->tirm', w_blocks, x_blocks, preferred_element_type=j...]
    unnamed x3 -> x1, local copies, waits for them, and re-layouts: 28.3 us -> 2.67 us
    concatenate x1 -> x0, other arithmetic: 23.8 us -> none  [local_product(): jnp.concatenate([w_near, w_next], axis=1)]
  transfers between devices with their start and end apart: 7 -> 0, of which waited for: 5 -> 0; matrix products, arithmetic and copies ran while one was open for 6% -> 0% of each run, Pallas kernels for 0% -> 0%
where the time goes in v1:
time: 223 us; the launch traced here: 221 us
  Pallas kernels  218 us (98%)
  local copies, waits for them, and re-layouts  2.67 us (1%)
    pallas_call x1, Pallas kernels, local_product(): pl.pallas_call(kernel, out_shape=jax.ShapeDtypeStruct(x_local.shape, jnp....  218 us

profile of v1, /device:TPU:2, one launch (start us, length us, event | category | flops | bytes accessed | tf_op | source)
XLA Modules:
  0.0 220.6 jit_solution(12690252268315891713)
XLA Ops:
  0.0 217.9 %gather_matmul.1 = bf16[3,256,1024]{2,1,0:T(8,128)(2,1)} custom-call(bf16[256,4096]{1,0:T(8,128)(2,1)} %w_ref.1, bf16[3,256,1024]{2,1,0:T(8,128)(2,1)} %x_ref.1), custom_call_target="tpu_custom_call" | custom-call | flops 25769803776 | tf_op jit(solution)/shard_map/gather_matmul/pallas_call | solution.py:301
  217.9 2.7 %copy.4 = bf16[3,256,1024]{2,1,0:T(8,128)(2,1)} copy(bf16[3,256,1024]{2,1,0:T(8,128)(2,1)} %gather_matmul.1) | data formatting | bytes 3145728

commit v2 on v0

v2 whole, which is shorter than its diff:
```python
import heapq

import jax
import jax.numpy as jnp
from jax import lax
from jax.experimental import pallas as pl
from jax.experimental.pallas import tpu as pltpu
from jax.sharding import PartitionSpec as P

MESH = pl.DeviceIdType.MESH
XS = 4
YS = 4
RHS = 3
CHUNKS = 6
POS = {0: 0, 1: 1, 3: 2, 2: 3}
GROUPS = ((0,), (1, 3), (2,))

A_UNIT_US = 11.3
X_UNIT_US = 5.65
T_UNIT_US = 3.0
D2D_US = 1.5
XCH_US = 2.9
HOP_US = 2.5
LOOKAHEAD_US = 9.0
BLOCK_US = 1.5


def a_sends(name):
    _, dx, dp, half, piece = name
    out = []

    def along_x():
        if dx == 0:
            out.append(("x+", ("A", 1, dp, half, piece)))
            out.append(("x-", ("A", 3, dp, half, piece)))
        elif dx == 1 and piece == 0:
            out.append(("x+", ("A", 2, dp, half, piece)))
        elif dx == 3 and piece == 1:
            out.append(("x-", ("A", 2, dp, half, piece)))

    if half == 0:
        if dp == 0:
            along_x()
            out.append(("ya", ("A", dx, 1, half, piece)))
    else:
        if dp == 0 and dx == 0:
            out.append(("ya", ("A", 0, 1, half, piece)))
        along_x()
    return out


def x_sends(name, depth_size):
    _, n, dz = name
    mid = depth_size // 2
    out = []
    if dz < mid:
        out.append(("z+", ("X", n, dz + 1) if dz + 1 < mid else ("XH", n, 0)))
    back = (depth_size - dz) % depth_size
    if back < mid:
        out.append(("z-", ("X", n, (dz - 1) % depth_size) if back + 1 < mid else ("XH", n, 1)))
    return out


def plan(depth_size):
    mid = depth_size // 2
    steps, heap, pools, link_free = [], [], {}, {}
    have = set()
    count = 0

    def arrive(when, name):
        nonlocal count
        heapq.heappush(heap, (when, count, name))
        count += 1

    def cost(name):
        if name[0] == "A":
            return A_UNIT_US
        return X_UNIT_US if name[0] == "X" else X_UNIT_US / 2

    def priority(name):
        if name[0] == "A":
            return (GROUPS.index(next(g for g in GROUPS if name[1] in g)), name[4])
        return (name[1],)

    def pump(now, ahead):
        for link, pool in pools.items():
            while pool and link_free.get(link, 0.0) < now + ahead:
                pool.sort()
                _, _, src, dst = pool.pop(0)
                begin = max(now, link_free.get(link, 0.0))
                link_free[link] = begin + cost(dst)
                arrive(begin + cost(dst) + HOP_US, dst)
                steps.append(("send", link, src, dst))

    def offer(link, src, dst):
        nonlocal count
        pools.setdefault(link, []).append((priority(dst), count, src, dst))
        count += 1

    def got(name, now):
        have.add(name)
        if name[0] == "A":
            for link, there in a_sends(name):
                offer(link, name, there)
        elif name[0] in ("T", "X"):
            unit = ("X", name[1], 0) if name[0] == "T" else name
            for link, there in x_sends(unit, depth_size):
                offer(link, unit, there)
            share(name[1], unit[2], now)
        elif name[0] == "XH" and ("XH", name[1], 1 - name[2]) in have:
            share(name[1], mid, now)

    def share(n, dz, now):
        steps.append(("share", n, dz))
        arrive(now + D2D_US + HOP_US, ("P", n, dz))

    now = 0.0
    for n in range(CHUNKS):
        arrive(HOP_US + 2.0 + (n + 1) * T_UNIT_US, ("T", n))
    steps.append(("a2a", 0))
    steps.append(("a2a", 1))
    for half, piece in ((0, 0), (1, 0), (0, 1), (1, 1)):
        got(("A", 0, 0, half, piece), now)
    pump(now, LOOKAHEAD_US)
    for n in range(2, CHUNKS):
        steps.append(("a2a", n))

    def needs(g, n):
        out = set(("A", dx, dp, half, piece) for dx in GROUPS[g] for dp in range(2) for half in range(2) for piece in range(2))
        out |= set(("P", n, dz) for dz in range(depth_size))
        out |= set(("X", n, dz) for dz in range(1, depth_size) if dz != mid) | {("T", n), ("XH", n, 0), ("XH", n, 1)}
        return out

    blocks = [(g, n) for n in range(CHUNKS) for g in range(len(GROUPS))]
    need = {b: needs(*b) for b in blocks}
    unsent = []
    while heap or blocks or unsent:
        while heap and heap[0][0] <= now:
            _, _, name = heapq.heappop(heap)
            if name[0] == "E":
                steps.append(("fin", name[1], name[2]))
                continue
            if name[0] != "P":
                steps.append(("wait", name))
            got(name, now)
            pump(now, LOOKAHEAD_US)
        ready = next((b for b in blocks if need[b] <= have), None)
        if ready is not None:
            blocks.remove(ready)
            g, n = ready
            spent = BLOCK_US * len(GROUPS[g])
            pump(now, LOOKAHEAD_US + spent)
            steps.append(("mm", g, n))
            now += spent
            steps.append(("xch", g, n))
            begin = max(now, link_free.get("yp", 0.0))
            link_free["yp"] = begin + XCH_US * len(GROUPS[g])
            arrive(link_free["yp"] + HOP_US, ("E", g, n))
        elif heap:
            now = max(now, heap[0][0])
        pump(now, LOOKAHEAD_US)
        if not heap and not blocks:
            break
    assert not blocks and not any(pools.values())
    return steps, now


def solution(mesh):
    depth_size = mesh.shape["depth"]
    mid = depth_size // 2
    steps, _ = plan(depth_size)

    def kernel(w_ref, x_ref, o_ref, a_all, x_all, acc, peer_acc, y_buf,
               a_ssem, a_rsem, x_ssem, x_rsem, d_ssem, d_rsem, t_ssem, t_rsem, e_ssem, e_rsem, y_ssem, y_rsem, l_sem):
        layer = lax.axis_index("depth")
        col = lax.axis_index("col")
        row = lax.axis_index("row")
        core = lax.rem(row, 2)
        xpos = row // 2
        rows, kcols = w_ref.shape
        unit = rows // 4
        hrows = rows // 2
        sub = x_ref.shape[2] // 4

        xh = xpos // 2
        yh = col // 2
        q = lax.rem((col + 1) // 2, 2)

        def col_of(high):
            return q + high * (3 - 2 * q)

        def at(x, y):
            return {"row": 2 * x + core, "col": y}

        src_col = col_of(1 - xh)
        own_out = lax.rem(xh + yh, 2)
        sources = [at(2 * yh + s, src_col) for s in range(2)]
        dests = [at(2 * (1 - yh) + b, col_of(xh)) for b in range(2)]
        makers = [(b, hi, at(2 * (1 - yh) + b, col_of(hi))) for b in range(2) for hi in range(2)]
        sibling = {"row": row + 1 - 2 * core}
        links = {
            "x+": {"row": lax.rem(row + 2, 2 * XS)},
            "x-": {"row": lax.rem(row + 6, 2 * XS)},
            "ya": {"col": col + 1 - 2 * lax.rem(col, 2)},
            "yp": {"col": 3 - col},
            "z+": {"depth": lax.rem(layer + 1, depth_size)},
            "z-": {"depth": lax.rem(layer + depth_size - 1, depth_size)},
        }

        def is_self(b, hi):
            same = (1 - lax.rem(xpos + b, 2)) * (1 - lax.rem(yh + hi, 2))
            return own_out * same

        barrier = pltpu.get_barrier_semaphore()
        partners = list(links.values()) + [sibling] + sources + dests
        for partner in partners:
            pl.semaphore_signal(barrier, inc=1, device_id=partner, device_id_type=MESH)
        for b, hi, maker in makers:
            @pl.when(is_self(b, hi) == 0)
            def _():
                pl.semaphore_signal(barrier, inc=1, device_id=maker, device_id_type=MESH)
        pl.semaphore_wait(barrier, len(partners) + 4 - own_out)

        sent = []

        def a_index(name):
            return ((name[1] * 2 + name[2]) * 2 + name[3]) * 2 + name[4]

        def a_slot(name):
            _, dx, dp, half, piece = name
            return a_all.at[dp, pl.ds(POS[dx] * rows + half * hrows + piece * unit, unit), :]

        def x_index(name):
            return name[1] * (depth_size + 1) + (depth_size if name == ("XH", name[1], 1) else mid if name[0] == "XH" else name[2])

        def x_rows(core_idx, dz):
            start = (core_idx * depth_size + lax.rem(layer + depth_size - dz, depth_size)) * rows
            return pl.ds(pl.multiple_of(start, rows), rows)

        def x_slot(name):
            if name[0] == "XH":
                return x_all.at[name[1], name[2], x_rows(core, mid), :]
            return x_all.at[name[1], :, x_rows(core, name[2]), :]

        def x_out(src, there):
            if there[0] == "XH":
                return x_all.at[there[1], there[2], x_rows(core, src[2]), :]
            return x_slot(src)

        def remote(src, dst, ssem, rsem, device):
            copy = pltpu.make_async_remote_copy(src_ref=src, dst_ref=dst, send_sem=ssem, recv_sem=rsem, device_id=device, device_id_type=MESH)
            copy.start()
            sent.append(copy)

        def landed(slot, rsem):
            pltpu.make_async_remote_copy(src_ref=slot, dst_ref=slot, send_sem=l_sem.at[0], recv_sem=rsem, device_id=sibling, device_id_type=MESH).wait_recv()

        def columns(n, half):
            return pl.ds(pl.multiple_of((half * 2 + n % 2) * sub, sub), sub)

        own_a = pltpu.make_async_copy(w_ref, a_all.at[0, pl.ds(0, rows), :], l_sem.at[1])

        def exchange_x(n):
            s = lax.rem(xpos + col_of(xh), 2)
            for b in range(2):
                src = x_ref.at[n // 2, :, columns(n, b)]
                remote(src, x_all.at[n, s, x_rows(core, 0), :], t_ssem.at[n * 2 + b], t_rsem.at[n * 2 + s], dests[b])

        def matmul(g, n):
            first, count = POS[GROUPS[g][0]], len(GROUPS[g])
            kstep = min(2048, kcols)
            per = kcols // kstep

            def body(idx, carry):
                dp = idx // per
                k0 = pl.multiple_of(lax.rem(idx, per) * kstep, kstep)
                lhs = a_all[dp, pl.ds(first * rows, count * rows), pl.ds(k0, kstep)]
                rhs = x_all[n, dp, pl.ds(k0, kstep), :]
                part = jnp.dot(lhs, rhs, preferred_element_type=jnp.float32)
                acc[n, pl.ds(first, count)] += part.reshape(count, rows, sub)
                return carry

            lax.fori_loop(0, 2 * per, body, 0)

        def span(g):
            return pl.ds(POS[GROUPS[g][0]], len(GROUPS[g]))

        def exchange_acc(g, n):
            src = acc.at[n, span(g), pl.ds(pl.multiple_of((1 - yh) * hrows, hrows), hrows), :]
            idx = n * len(GROUPS) + g
            remote(src, peer_acc.at[n, span(g)], e_ssem.at[idx], e_rsem.at[idx], links["yp"])

        def out_slot(n, half, hi):
            return o_ref.at[n // 2, pl.ds(pl.multiple_of(hi * hrows, hrows), hrows), columns(n, half)]

        def y_sem(n, half, hi):
            return n * 4 + half * 2 + hi

        def finish(g, n):
            idx = n * len(GROUPS) + g
            landed(peer_acc.at[n, span(g)], e_rsem.at[idx])
            mine = pl.ds(pl.multiple_of(yh * hrows, hrows), hrows)
            y_buf[n, span(g)] = (acc[n, span(g), mine, :] + peer_acc[n, span(g)]).astype(y_buf.dtype)
            half = lax.rem(xpos, 2)
            for dx in GROUPS[g]:
                src = y_buf.at[n, POS[dx]]
                dst = out_slot(n, half, yh)
                ssem = y_ssem.at[n * 4 + dx]
                target = at(lax.rem(xpos + XS - dx, XS), src_col)

                def go():
                    pltpu.make_async_remote_copy(src_ref=src, dst_ref=dst, send_sem=ssem, recv_sem=y_rsem.at[y_sem(n, half, yh)], device_id=target, device_id_type=MESH).start()

                if dx == 0:
                    pl.when(own_out == 1)(lambda: pltpu.make_async_copy(src, dst, ssem).start())
                    pl.when(own_out == 0)(go)
                else:
                    go()

        waited = set()
        for step in steps:
            if step[0] == "a2a":
                exchange_x(step[1])
                if step[1] == CHUNKS - 1:
                    own_a.start()
                    acc[...] = jnp.zeros_like(acc)
            elif step[0] == "send":
                _, link, src, dst = step
                if dst[0] == "A":
                    if src[1:3] == (0, 0):
                        ref = w_ref.at[pl.ds(src[3] * hrows + src[4] * unit, unit), :]
                    else:
                        ref = a_slot(src)
                    idx = a_index(dst)
                    remote(ref, a_slot(dst), a_ssem.at[idx], a_rsem.at[idx], links[link])
                else:
                    idx = x_index(dst)
                    ref = x_out(src, dst)
                    remote(ref, ref, x_ssem.at[idx], x_rsem.at[idx], links[link])
            elif step[0] == "wait":
                name = step[1]
                if name[0] == "A":
                    landed(a_slot(name), a_rsem.at[a_index(name)])
                elif name[0] == "T":
                    for s in range(2):
                        landed(x_all.at[name[1], s, x_rows(core, 0), :], t_rsem.at[name[1] * 2 + s])
                else:
                    landed(x_slot(name), x_rsem.at[x_index(name)])
            elif step[0] == "share":
                _, n, dz = step
                slot = x_all.at[n, :, x_rows(core, dz), :]
                remote(slot, slot, d_ssem.at[n * depth_size + dz], d_rsem.at[n * depth_size + dz], sibling)
            elif step[0] == "mm":
                _, g, n = step
                if "a" not in waited:
                    waited.add("a")
                    own_a.wait()
                if n not in waited:
                    waited.add(n)
                    for dz in range(depth_size):
                        landed(x_all.at[n, :, x_rows(1 - core, dz), :], d_rsem.at[n * depth_size + dz])
                matmul(g, n)
            elif step[0] == "xch":
                exchange_acc(step[1], step[2])
            else:
                finish(step[1], step[2])

        for n in range(CHUNKS):
            for b in range(2):
                for hi in range(2):
                    slot = out_slot(n, b, hi)
                    sem = y_rsem.at[y_sem(n, b, hi)]
                    pl.when(is_self(b, hi) == 0)(lambda: landed(slot, sem))
            for dx in range(XS):
                src = y_buf.at[n, POS[dx]]
                pltpu.make_async_copy(src, src, y_ssem.at[n * 4 + dx]).wait()
        for copy in sent:
            copy.wait_send()

    def local_product(w_local, x_local):
        rows, kcols = w_local.shape
        sub = x_local.shape[2] // 4
        dma = pltpu.SemaphoreType.DMA

        def sems(size):
            return [dma((size,)), dma((size,))]

        return pl.pallas_call(
            kernel,
            out_shape=jax.ShapeDtypeStruct(x_local.shape, jnp.bfloat16),
            in_specs=[pl.BlockSpec(memory_space=pl.ANY)] * 2,
            out_specs=pl.BlockSpec(memory_space=pl.ANY),
            scratch_shapes=[
                pltpu.VMEM((2, XS * rows, kcols), jnp.bfloat16),
                pltpu.VMEM((CHUNKS, 2, kcols, sub), jnp.bfloat16),
                pltpu.VMEM((CHUNKS, XS, rows, sub), jnp.float32),
                pltpu.VMEM((CHUNKS, XS, rows // 2, sub), jnp.float32),
                pltpu.VMEM((CHUNKS, XS, rows // 2, sub), jnp.bfloat16),
                *sems(32), *sems(CHUNKS * (depth_size + 1)), *sems(CHUNKS * depth_size),
                *sems(CHUNKS * 2), *sems(CHUNKS * len(GROUPS)), *sems(CHUNKS * 4), dma((2,)),
            ],
            compiler_params=pltpu.CompilerParams(collective_id=0, has_side_effects=True, vmem_limit_bytes=67043328),
            cost_estimate=pl.CostEstimate(flops=2 * XS * rows * 2 * kcols * CHUNKS * sub, bytes_accessed=0, transcendentals=0),
            name="gather_matmul",
        )(w_local, x_local)

    return jax.shard_map(local_product, mesh=mesh, in_specs=(P(("row", "depth"), "col"), P(None, ("row", "depth"), "col")), out_specs=P(None, ("row", "depth"), "col"), check_vma=False)
```

time: 1280 us -> 226 us (0.18)
  waiting for transfers between devices: 1080 us -> 0 us
  Pallas kernels: 0 us -> 222 us
  starting transfers between devices: 58.4 us -> 0 us
  local copies, waits for them, and re-layouts: 56.5 us -> 2.67 us
  matrix products: 35.1 us -> 0 us
  other arithmetic: 25.9 us -> 0 us
  between operations: 13.2 us -> 0.01 us
    ppermute x4 -> x0, waiting for transfers between devices: 530 us -> none  [the longest x1 361 us: local_product(): w_near = lax.ppermute(w_layer, ALL_AXES, perm_a_near)]
    all_gather x2 -> x0, waiting for transfers between devices: 302 us -> none  [the longest x1 177 us: local_product(): w_layer = lax.all_gather(w_local, 'depth', axis=0, tiled=True)]
    reduce_scatter x1 -> x0, waiting for transfers between devices: 248 us -> none  [local_product(): lax.psum_scatter(partial_sum, 'depth', scatter_dimension=1, tiled=True)]
    pallas_call x0 -> x1, Pallas kernels: none -> 222 us  [local_product(): pl.pallas_call(kernel, out_shape=jax.ShapeDtypeStruct(x_local.shape, jnp....]
    ppermute x4 -> x0, starting transfers between devices: 58.3 us -> none  [the longest x2 50.4 us: local_product(): lax.ppermute(x_layer[piece_idx], ALL_AXES, perm_x_pieces[piece_idx])]
    dot_general x1 -> x0, matrix products: 35.1 us -> none  [local_product(): jnp.einsum('tik,tkrm->tirm', w_blocks, x_blocks, preferred_element_type=j...]
    unnamed x3 -> x1, local copies, waits for them, and re-layouts: 28.3 us -> 2.67 us
    concatenate x1 -> x0, other arithmetic: 23.8 us -> none  [local_product(): jnp.concatenate([w_near, w_next], axis=1)]
  transfers between devices with their start and end apart: 7 -> 0, of which waited for: 5 -> 0; matrix products, arithmetic and copies ran while one was open for 6% -> 0% of each run, Pallas kernels for 0% -> 0%
where the time goes in v2:
time: 226 us; the launch traced here: 224 us
  Pallas kernels  222 us (98%)
  local copies, waits for them, and re-layouts  2.67 us (1%)
    pallas_call x1, Pallas kernels, local_product(): pl.pallas_call(kernel, out_shape=jax.ShapeDtypeStruct(x_local.shape, jnp....  222 us

profile of v2, /device:TPU:2, one launch (start us, length us, event | category | flops | bytes accessed | tf_op | source)
XLA Modules:
  0.0 224.2 jit_solution(11791043749651282185)
XLA Ops:
  0.0 221.5 %gather_matmul.1 = bf16[3,256,1024]{2,1,0:T(8,128)(2,1)} custom-call(bf16[256,4096]{1,0:T(8,128)(2,1)} %w_ref.1, bf16[3,256,1024]{2,1,0:T(8,128)(2,1)} %x_ref.1), custom_call_target="tpu_custom_call" | custom-call | flops 25769803776 | tf_op jit(solution)/shard_map/gather_matmul/pallas_call | solution.py:388
  221.5 2.7 %copy.4 = bf16[3,256,1024]{2,1,0:T(8,128)(2,1)} copy(bf16[3,256,1024]{2,1,0:T(8,128)(2,1)} %gather_matmul.1) | data formatting | bytes 3145728

commit v3 on v2

--- a/solution.py
+++ b/solution.py
@@ -11,18 +11,20 @@
 XS = 4
 YS = 4
 RHS = 3
-CHUNKS = 6
+CHUNKS = 2 * RHS
+ORDER = (0, 1, 2, 3, 4, 5)
 POS = {0: 0, 1: 1, 3: 2, 2: 3}
-GROUPS = ((0,), (1, 3), (2,))
+READY = ((0,), (1,), (3,), (2,))
 
 A_UNIT_US = 11.3
 X_UNIT_US = 5.65
-T_UNIT_US = 3.0
+T_AT_US = (16.0, 27.0, 38.0, 8.0, 30.0, 60.0)
 D2D_US = 1.5
-XCH_US = 2.9
+XCH_US = 5.65
 HOP_US = 2.5
-LOOKAHEAD_US = 9.0
-BLOCK_US = 1.5
+LOOKAHEAD_US = 2.0
+BLOCK_US = 1.4
+FIN_US = 0.3
 
 
 def a_sends(name):
@@ -79,8 +81,8 @@
 
     def priority(name):
         if name[0] == "A":
-            return (GROUPS.index(next(g for g in GROUPS if name[1] in g)), name[4])
-        return (name[1],)
+            return (next(i for i, g in enumerate(READY) if name[1] in g), name[4])
+        return (ORDER.index(name[1]),)
 
     def pump(now, ahead):
         for link, pool in pools.items():
@@ -116,52 +118,73 @@
 
     now = 0.0
     for n in range(CHUNKS):
-        arrive(HOP_US + 2.0 + (n + 1) * T_UNIT_US, ("T", n))
+        arrive(T_AT_US[n], ("T", n))
     steps.append(("a2a", 0))
-    steps.append(("a2a", 1))
     for half, piece in ((0, 0), (1, 0), (0, 1), (1, 1)):
         got(("A", 0, 0, half, piece), now)
     pump(now, LOOKAHEAD_US)
-    for n in range(2, CHUNKS):
-        steps.append(("a2a", n))
-
-    def needs(g, n):
-        out = set(("A", dx, dp, half, piece) for dx in GROUPS[g] for dp in range(2) for half in range(2) for piece in range(2))
-        out |= set(("P", n, dz) for dz in range(depth_size))
-        out |= set(("X", n, dz) for dz in range(1, depth_size) if dz != mid) | {("T", n), ("XH", n, 0), ("XH", n, 1)}
-        return out
-
-    blocks = [(g, n) for n in range(CHUNKS) for g in range(len(GROUPS))]
-    need = {b: needs(*b) for b in blocks}
-    unsent = []
-    while heap or blocks or unsent:
+    for r in range(1, RHS):
+        steps.append(("a2a", r))
+
+    def a_need(pos):
+        return set(("A", dx, dp, half, piece) for dx in POS if POS[dx] == pos for dp in range(2) for half in range(2) for piece in range(2))
+
+    def x_need(n):
+        out = set(("P", n, dz) for dz in range(depth_size))
+        return out | set(("X", n, dz) for dz in range(1, depth_size) if dz != mid) | {("T", n), ("XH", n, 0), ("XH", n, 1)}
+
+    left = [(n, pos) for n in ORDER for pos in range(XS)]
+    made, arrived, finished = set(), set(), set()
+
+    def next_block():
+        for n in ORDER:
+            run = [pos for pos in range(XS) if (n, pos) in left and a_need(pos) <= have]
+            if run and x_need(n) <= have:
+                stop = run[0] + 1
+                while stop in run:
+                    stop += 1
+                return n, run[0], stop
+        return None
+
+    def finish_ready():
+        for r in range(RHS):
+            for pos in range(XS):
+                if (r, pos) in arrived and (RHS + r, pos) in made and (r, pos) not in finished:
+                    finished.add((r, pos))
+                    steps.append(("fin", r, pos))
+
+    while heap or left:
         while heap and heap[0][0] <= now:
             _, _, name = heapq.heappop(heap)
             if name[0] == "E":
-                steps.append(("fin", name[1], name[2]))
+                _, n, lo, hi = name
+                steps.append(("peer", n, lo, hi))
+                arrived |= set((n, pos) for pos in range(lo, hi))
+                finish_ready()
                 continue
             if name[0] != "P":
                 steps.append(("wait", name))
             got(name, now)
             pump(now, LOOKAHEAD_US)
-        ready = next((b for b in blocks if need[b] <= have), None)
-        if ready is not None:
-            blocks.remove(ready)
-            g, n = ready
-            spent = BLOCK_US * len(GROUPS[g])
+        block = next_block()
+        if block is not None:
+            n, lo, hi = block
+            left = [b for b in left if b[0] != n or not lo <= b[1] < hi]
+            spent = BLOCK_US * (hi - lo)
             pump(now, LOOKAHEAD_US + spent)
-            steps.append(("mm", g, n))
+            steps.append(("mm", n, lo, hi))
             now += spent
-            steps.append(("xch", g, n))
-            begin = max(now, link_free.get("yp", 0.0))
-            link_free["yp"] = begin + XCH_US * len(GROUPS[g])
-            arrive(link_free["yp"] + HOP_US, ("E", g, n))
+            made |= set((n, pos) for pos in range(lo, hi))
+            if n < RHS:
+                steps.append(("xch", n, lo, hi))
+                begin = max(now, link_free.get("yp", 0.0))
+                link_free["yp"] = begin + XCH_US * (hi - lo)
+                arrive(link_free["yp"] + HOP_US, ("E", n, lo, hi))
+            finish_ready()
         elif heap:
             now = max(now, heap[0][0])
         pump(now, LOOKAHEAD_US)
-        if not heap and not blocks:
-            break
-    assert not blocks and not any(pools.values())
+    assert not any(pools.values()) and len(finished) == RHS * XS
     return steps, now
 
 
@@ -184,19 +207,12 @@
 
         xh = xpos // 2
         yh = col // 2
-        q = lax.rem((col + 1) // 2, 2)
-
-        def col_of(high):
-            return q + high * (3 - 2 * q)
-
-        def at(x, y):
-            return {"row": 2 * x + core, "col": y}
-
-        src_col = col_of(1 - xh)
-        own_out = lax.rem(xh + yh, 2)
-        sources = [at(2 * yh + s, src_col) for s in range(2)]
-        dests = [at(2 * (1 - yh) + b, col_of(xh)) for b in range(2)]
-        makers = [(b, hi, at(2 * (1 - yh) + b, col_of(hi))) for b in range(2) for hi in range(2)]
+        cross = lax.rem(xh + yh, 2)
+        x_col = col + cross * (3 - 2 * col)
+
+        def at(hops, y):
+            return {"row": lax.rem(row + 2 * hops, 2 * XS), "col": y}
+
         sibling = {"row": row + 1 - 2 * core}
         links = {
             "x+": {"row": lax.rem(row + 2, 2 * XS)},
@@ -207,19 +223,12 @@
             "z-": {"depth": lax.rem(layer + depth_size - 1, depth_size)},
         }
 
-        def is_self(b, hi):
-            same = (1 - lax.rem(xpos + b, 2)) * (1 - lax.rem(yh + hi, 2))
-            return own_out * same
-
         barrier = pltpu.get_barrier_semaphore()
-        partners = list(links.values()) + [sibling] + sources + dests
+        partners = [links["ya"], links["z+"], links["z-"], sibling]
+        partners += [at(hops, col) for hops in range(1, XS)] + [at(hops, 3 - col) for hops in range(XS)]
         for partner in partners:
             pl.semaphore_signal(barrier, inc=1, device_id=partner, device_id_type=MESH)
-        for b, hi, maker in makers:
-            @pl.when(is_self(b, hi) == 0)
-            def _():
-                pl.semaphore_signal(barrier, inc=1, device_id=maker, device_id_type=MESH)
-        pl.semaphore_wait(barrier, len(partners) + 4 - own_out)
+        pl.semaphore_wait(barrier, len(partners))
 
         sent = []
 
@@ -255,73 +264,64 @@
         def landed(slot, rsem):
             pltpu.make_async_remote_copy(src_ref=slot, dst_ref=slot, send_sem=l_sem.at[0], recv_sem=rsem, device_id=sibling, device_id_type=MESH).wait_recv()
 
-        def columns(n, half):
-            return pl.ds(pl.multiple_of((half * 2 + n % 2) * sub, sub), sub)
+        def columns(block):
+            return pl.ds(pl.multiple_of(block * sub, sub), sub)
 
         own_a = pltpu.make_async_copy(w_ref, a_all.at[0, pl.ds(0, rows), :], l_sem.at[1])
 
-        def exchange_x(n):
-            s = lax.rem(xpos + col_of(xh), 2)
-            for b in range(2):
-                src = x_ref.at[n // 2, :, columns(n, b)]
-                remote(src, x_all.at[n, s, x_rows(core, 0), :], t_ssem.at[n * 2 + b], t_rsem.at[n * 2 + s], dests[b])
-
-        def matmul(g, n):
-            first, count = POS[GROUPS[g][0]], len(GROUPS[g])
+        def exchange_x(r):
+            s = lax.rem(xpos + x_col, 2)
+            n = (1 - cross) * RHS + r
+            for hops in (1, 3, 2, 0):
+                src = x_ref.at[r, :, columns(lax.rem(xpos + hops, XS))]
+                dst = x_all.at[n, s, x_rows(core, 0), :]
+                ssem, rsem = t_ssem.at[r * XS + hops], t_rsem.at[n * 2 + s]
+                if hops == 0:
+                    pl.when(cross == 0)(lambda: pltpu.make_async_copy(src, dst, rsem).start())
+
+                    @pl.when(cross == 1)
+                    def _():
+                        pltpu.make_async_remote_copy(src_ref=src, dst_ref=dst, send_sem=ssem, recv_sem=rsem, device_id=at(0, 3 - col), device_id_type=MESH).start()
+                else:
+                    remote(src, dst, ssem, rsem, at(hops, x_col))
+
+        def matmul(n, lo, hi):
             kstep = min(2048, kcols)
             per = kcols // kstep
 
             def body(idx, carry):
                 dp = idx // per
                 k0 = pl.multiple_of(lax.rem(idx, per) * kstep, kstep)
-                lhs = a_all[dp, pl.ds(first * rows, count * rows), pl.ds(k0, kstep)]
+                lhs = a_all[dp, pl.ds(lo * rows, (hi - lo) * rows), pl.ds(k0, kstep)]
                 rhs = x_all[n, dp, pl.ds(k0, kstep), :]
                 part = jnp.dot(lhs, rhs, preferred_element_type=jnp.float32)
-                acc[n, pl.ds(first, count)] += part.reshape(count, rows, sub)
+                acc[n, pl.ds(lo, hi - lo)] += part.reshape(hi - lo, rows, sub)
                 return carry
 
             lax.fori_loop(0, 2 * per, body, 0)
 
-        def span(g):
-            return pl.ds(POS[GROUPS[g][0]], len(GROUPS[g]))
-
-        def exchange_acc(g, n):
-            src = acc.at[n, span(g), pl.ds(pl.multiple_of((1 - yh) * hrows, hrows), hrows), :]
-            idx = n * len(GROUPS) + g
-            remote(src, peer_acc.at[n, span(g)], e_ssem.at[idx], e_rsem.at[idx], links["yp"])
-
-        def out_slot(n, half, hi):
-            return o_ref.at[n // 2, pl.ds(pl.multiple_of(hi * hrows, hrows), hrows), columns(n, half)]
-
-        def y_sem(n, half, hi):
-            return n * 4 + half * 2 + hi
-
-        def finish(g, n):
-            idx = n * len(GROUPS) + g
-            landed(peer_acc.at[n, span(g)], e_rsem.at[idx])
-            mine = pl.ds(pl.multiple_of(yh * hrows, hrows), hrows)
-            y_buf[n, span(g)] = (acc[n, span(g), mine, :] + peer_acc[n, span(g)]).astype(y_buf.dtype)
-            half = lax.rem(xpos, 2)
-            for dx in GROUPS[g]:
-                src = y_buf.at[n, POS[dx]]
-                dst = out_slot(n, half, yh)
-                ssem = y_ssem.at[n * 4 + dx]
-                target = at(lax.rem(xpos + XS - dx, XS), src_col)
-
-                def go():
-                    pltpu.make_async_remote_copy(src_ref=src, dst_ref=dst, send_sem=ssem, recv_sem=y_rsem.at[y_sem(n, half, yh)], device_id=target, device_id_type=MESH).start()
-
-                if dx == 0:
-                    pl.when(own_out == 1)(lambda: pltpu.make_async_copy(src, dst, ssem).start())
-                    pl.when(own_out == 0)(go)
-                else:
-                    go()
+        def exchange_acc(n, lo, hi):
+            span = pl.ds(lo, hi - lo)
+            remote(acc.at[n, span], peer_acc.at[n, span], e_ssem.at[n * XS + lo], e_rsem.at[n * XS + lo], links["yp"])
+
+        local = []
+
+        def finish(r, pos):
+            dx = next(d for d in POS if POS[d] == pos)
+            y_buf[r, pos] = (acc[RHS + r, pos] + peer_acc[r, pos]).astype(y_buf.dtype)
+            src, dst = y_buf.at[r, pos], o_ref.at[r, :, columns(xpos)]
+            if dx == 0:
+                copy = pltpu.make_async_copy(src, dst, y_ssem.at[r * XS])
+                copy.start()
+                local.append(copy)
+            else:
+                remote(src, dst, y_ssem.at[r * XS + dx], y_rsem.at[r * XS + dx], at(XS - dx, col))
 
         waited = set()
         for step in steps:
             if step[0] == "a2a":
                 exchange_x(step[1])
-                if step[1] == CHUNKS - 1:
+                if step[1] == RHS - 1:
                     own_a.start()
                     acc[...] = jnp.zeros_like(acc)
             elif step[0] == "send":
@@ -351,7 +351,7 @@
                 slot = x_all.at[n, :, x_rows(core, dz), :]
                 remote(slot, slot, d_ssem.at[n * depth_size + dz], d_rsem.at[n * depth_size + dz], sibling)
             elif step[0] == "mm":
-                _, g, n = step
+                _, n, lo, hi = step
                 if "a" not in waited:
                     waited.add("a")
                     own_a.wait()
@@ -359,21 +359,25 @@
                     waited.add(n)
                     for dz in range(depth_size):
                         landed(x_all.at[n, :, x_rows(1 - core, dz), :], d_rsem.at[n * depth_size + dz])
-                matmul(g, n)
+                matmul(n, lo, hi)
             elif step[0] == "xch":
-                exchange_acc(step[1], step[2])
+                exchange_acc(*step[1:])
+            elif step[0] == "peer":
+                _, n, lo, hi = step
+                landed(peer_acc.at[n, pl.ds(lo, hi - lo)], e_rsem.at[n * XS + lo])
             else:
                 finish(step[1], step[2])
 
-        for n in range(CHUNKS):
-            for b in range(2):
-                for hi in range(2):
-                    slot = out_slot(n, b, hi)
-                    sem = y_rsem.at[y_sem(n, b, hi)]
-                    pl.when(is_self(b, hi) == 0)(lambda: landed(slot, sem))
-            for dx in range(XS):
-                src = y_buf.at[n, POS[dx]]
-                pltpu.make_async_copy(src, src, y_ssem.at[n * 4 + dx]).wait()
+        for r in range(RHS):
+            for dx in range(1, XS):
+                landed(o_ref.at[r, :, columns(lax.rem(xpos + dx, XS))], y_rsem.at[r * XS + dx])
+
+            @pl.when(cross == 1)
+            def _():
+                src = x_ref.at[r, :, columns(xpos)]
+                pltpu.make_async_remote_copy(src_ref=src, dst_ref=src, send_sem=t_ssem.at[r * XS], recv_sem=t_rsem.at[0], device_id=at(0, 3 - col), device_id_type=MESH).wait_send()
+        for copy in local:
+            copy.wait()
         for copy in sent:
             copy.wait_send()
 
@@ -394,10 +398,10 @@
                 pltpu.VMEM((2, XS * rows, kcols), jnp.bfloat16),
                 pltpu.VMEM((CHUNKS, 2, kcols, sub), jnp.bfloat16),
                 pltpu.VMEM((CHUNKS, XS, rows, sub), jnp.float32),
-                pltpu.VMEM((CHUNKS, XS, rows // 2, sub), jnp.float32),
-                pltpu.VMEM((CHUNKS, XS, rows // 2, sub), jnp.bfloat16),
+                pltpu.VMEM((RHS, XS, rows, sub), jnp.float32),
+                pltpu.VMEM((RHS, XS, rows, sub), jnp.bfloat16),
                 *sems(32), *sems(CHUNKS * (depth_size + 1)), *sems(CHUNKS * depth_size),
-                *sems(CHUNKS * 2), *sems(CHUNKS * len(GROUPS)), *sems(CHUNKS * 4), dma((2,)),
+                dma((RHS * XS,)), dma((CHUNKS * 2,)), *sems(RHS * XS), *sems(RHS * XS), dma((2,)),
             ],
             compiler_params=pltpu.CompilerParams(collective_id=0, has_side_effects=True, vmem_limit_bytes=67043328),
             cost_estimate=pl.CostEstimate(flops=2 * XS * rows * 2 * kcols * CHUNKS * sub, bytes_accessed=0, transcendentals=0),

time: 226 us -> 181 us (0.80)
  Pallas kernels: 222 us -> 178 us
    pallas_call x1, Pallas kernels: 222 us -> 178 us  [local_product(): pl.pallas_call(kernel, out_shape=jax.ShapeDtypeStruct(x_local.shape, jnp....]
where the time goes in v3:
time: 181 us
  Pallas kernels  178 us (98%)
  local copies, waits for them, and re-layouts  2.67 us (1%)
    pallas_call x1, Pallas kernels, local_product(): pl.pallas_call(kernel, out_shape=jax.ShapeDtypeStruct(x_local.shape, jnp....  178 us

profile of v3, /device:TPU:2, one launch (start us, length us, event | category | flops | bytes accessed | tf_op | source)
XLA Modules:
  0.0 180.6 jit_solution(6597737257020193962)
XLA Ops:
  0.0 178.0 %gather_matmul.1 = bf16[3,256,1024]{2,1,0:T(8,128)(2,1)} custom-call(bf16[256,4096]{1,0:T(8,128)(2,1)} %w_ref.1, bf16[3,256,1024]{2,1,0:T(8,128)(2,1)} %x_ref.1), custom_call_target="tpu_custom_call" | custom-call | flops 25769803776 | tf_op jit(solution)/shard_map/gather_matmul/pallas_call | solution.py:392
  178.0 2.7 %copy.4 = bf16[3,256,1024]{2,1,0:T(8,128)(2,1)} copy(bf16[3,256,1024]{2,1,0:T(8,128)(2,1)} %gather_matmul.1) | data formatting | bytes 3145728

commit v4 on v3

--- a/solution.py
+++ b/solution.py
@@ -18,13 +18,18 @@
 
 A_UNIT_US = 11.3
 X_UNIT_US = 5.65
-T_AT_US = (16.0, 27.0, 38.0, 8.0, 30.0, 60.0)
+T_X_US = 5.65
+T_Y_US = 11.3
+HOLD_US = (0.0, 0.0, 0.0, 0.0, 30.0, 60.0)
+A2A_AT_US = (0.0, 0.0, 0.0)
+OUT_US = 2.8
 D2D_US = 1.5
 XCH_US = 5.65
 HOP_US = 2.5
 LOOKAHEAD_US = 2.0
 BLOCK_US = 1.4
-FIN_US = 0.3
+LATE_US = 0.0
+LATE_E_US = 0.0
 
 
 def a_sends(name):
@@ -71,6 +76,10 @@
 
     def arrive(when, name):
         nonlocal count
+        if name[0] == "E":
+            when += LATE_E_US
+        elif name[0] == "P" or name[0] == "A" and not a_sends(name):
+            when += LATE_US
         heapq.heappush(heap, (when, count, name))
         count += 1
 
@@ -117,14 +126,23 @@
         arrive(now + D2D_US + HOP_US, ("P", n, dz))
 
     now = 0.0
-    for n in range(CHUNKS):
-        arrive(T_AT_US[n], ("T", n))
-    steps.append(("a2a", 0))
+
+    def take(link, when, spent):
+        link_free[link] = max(when, link_free.get(link, 0.0)) + spent
+        return link_free[link]
+
+    def exchange(r):
+        steps.append(("a2a", r))
+        near = max(take("x+", now, T_X_US), take("x-", now, T_X_US)) + HOP_US
+        arrive(max(near, HOLD_US[RHS + r]), ("T", RHS + r))
+        arrive(max(take("yp", now, T_Y_US) + HOP_US + 1.0, near, HOLD_US[r]), ("T", r))
+
+    exchange(0)
     for half, piece in ((0, 0), (1, 0), (0, 1), (1, 1)):
         got(("A", 0, 0, half, piece), now)
     pump(now, LOOKAHEAD_US)
     for r in range(1, RHS):
-        steps.append(("a2a", r))
+        arrive(A2A_AT_US[r], ("a2a", r))
 
     def a_need(pos):
         return set(("A", dx, dp, half, piece) for dx in POS if POS[dx] == pos for dp in range(2) for half in range(2) for piece in range(2))
@@ -135,6 +153,7 @@
 
     left = [(n, pos) for n in ORDER for pos in range(XS)]
     made, arrived, finished = set(), set(), set()
+    done = [0.0]
 
     def next_block():
         for n in ORDER:
@@ -152,10 +171,15 @@
                 if (r, pos) in arrived and (RHS + r, pos) in made and (r, pos) not in finished:
                     finished.add((r, pos))
                     steps.append(("fin", r, pos))
+                    for link in (("x-",), ("x+",), ("x+", "x-"))[pos - 1] if pos else ():
+                        done[0] = max(done[0], take(link, now, OUT_US) + HOP_US)
 
     while heap or left:
         while heap and heap[0][0] <= now:
             _, _, name = heapq.heappop(heap)
+            if name[0] == "a2a":
+                exchange(name[1])
+                continue
             if name[0] == "E":
                 _, n, lo, hi = name
                 steps.append(("peer", n, lo, hi))
@@ -185,7 +209,7 @@
             now = max(now, heap[0][0])
         pump(now, LOOKAHEAD_US)
     assert not any(pools.values()) and len(finished) == RHS * XS
-    return steps, now
+    return steps, max(now, done[0])
 
 
 def solution(mesh):

time: 181 us -> 166 us (0.917)
  Pallas kernels: 178 us -> 163 us
    pallas_call x1, Pallas kernels: 178 us -> 163 us  [local_product(): pl.pallas_call(kernel, out_shape=jax.ShapeDtypeStruct(x_local.shape, jnp....]
where the time goes in v4:
time: 166 us
  Pallas kernels  163 us (98%)
  local copies, waits for them, and re-layouts  2.67 us (2%)
    pallas_call x1, Pallas kernels, local_product(): pl.pallas_call(kernel, out_shape=jax.ShapeDtypeStruct(x_local.shape, jnp....  163 us

profile of v4, /device:TPU:2, one launch (start us, length us, event | category | flops | bytes accessed | tf_op | source)
XLA Modules:
  0.0 165.7 jit_solution(16104357527879700135)
XLA Ops:
  0.0 163.0 %gather_matmul.1 = bf16[3,256,1024]{2,1,0:T(8,128)(2,1)} custom-call(bf16[256,4096]{1,0:T(8,128)(2,1)} %w_ref.1, bf16[3,256,1024]{2,1,0:T(8,128)(2,1)} %x_ref.1), custom_call_target="tpu_custom_call" | custom-call | flops 25769803776 | tf_op jit(solution)/shard_map/gather_matmul/pallas_call | solution.py:416
  163.0 2.7 %copy.4 = bf16[3,256,1024]{2,1,0:T(8,128)(2,1)} copy(bf16[3,256,1024]{2,1,0:T(8,128)(2,1)} %gather_matmul.1) | data formatting | bytes 3145728

commit v5 on v4

--- a/solution.py
+++ b/solution.py
@@ -13,21 +13,27 @@
 RHS = 3
 CHUNKS = 2 * RHS
 ORDER = (0, 1, 2, 3, 4, 5)
+BLOCKS = 2 * XS
+FINE = 8
 POS = {0: 0, 1: 1, 3: 2, 2: 3}
-READY = ((0,), (1,), (3,), (2,))
+READY = ((0,), (1,), (2,), (3,))
 
 A_UNIT_US = 11.3
 X_UNIT_US = 5.65
 T_X_US = 5.65
 T_Y_US = 11.3
-HOLD_US = (0.0, 0.0, 0.0, 0.0, 30.0, 60.0)
-A2A_AT_US = (0.0, 0.0, 0.0)
-OUT_US = 2.8
+HOLD_US = (0.0, 0.0, 0.0, 9, 55, 66)
+A2A_AT_US = (0.0, 0.0, 24.4)
+OUT_US = 1.41
 D2D_US = 1.5
-XCH_US = 5.65
+XCH_US = 2.83
 HOP_US = 2.5
-LOOKAHEAD_US = 2.0
-BLOCK_US = 1.4
+AHEAD_A_US = 2.4
+AHEAD_X_US = 2.5
+A_WEIGHTS = (1.3, 0.06, 0.78, -0.71)
+X_WEIGHTS = (0.4, 0.33)
+BLOCK_US = 0.55
+BLOCK0_US = 0.4
 LATE_US = 0.0
 LATE_E_US = 0.0
 
@@ -90,11 +96,14 @@
 
     def priority(name):
         if name[0] == "A":
-            return (next(i for i, g in enumerate(READY) if name[1] in g), name[4])
-        return (ORDER.index(name[1]),)
-
-    def pump(now, ahead):
+            parts = (next(i for i, g in enumerate(READY) if name[1] in g), name[3], name[2], name[4])
+            return sum(w * p for w, p in zip(A_WEIGHTS, parts))
+        away = mid if name[0] == "XH" else min(name[2], depth_size - name[2])
+        return X_WEIGHTS[0] * ORDER.index(name[1]) + X_WEIGHTS[1] * away
+
+    def pump(now, spent):
         for link, pool in pools.items():
+            ahead = spent + (AHEAD_X_US if link[0] == "z" else AHEAD_A_US)
             while pool and link_free.get(link, 0.0) < now + ahead:
                 pool.sort()
                 _, _, src, dst = pool.pop(0)
@@ -140,38 +149,43 @@
     exchange(0)
     for half, piece in ((0, 0), (1, 0), (0, 1), (1, 1)):
         got(("A", 0, 0, half, piece), now)
-    pump(now, LOOKAHEAD_US)
+    pump(now, 0.0)
     for r in range(1, RHS):
         arrive(A2A_AT_US[r], ("a2a", r))
 
     def a_need(pos):
-        return set(("A", dx, dp, half, piece) for dx in POS if POS[dx] == pos for dp in range(2) for half in range(2) for piece in range(2))
+        return set(("A", dx, dp, pos % 2, piece) for dx in POS if POS[dx] == pos // 2 for dp in range(2) for piece in range(2))
 
     def x_need(n):
         out = set(("P", n, dz) for dz in range(depth_size))
         return out | set(("X", n, dz) for dz in range(1, depth_size) if dz != mid) | {("T", n), ("XH", n, 0), ("XH", n, 1)}
 
-    left = [(n, pos) for n in ORDER for pos in range(XS)]
+    left = [(n, pos) for n in ORDER for pos in range(BLOCKS)]
     made, arrived, finished = set(), set(), set()
     done = [0.0]
 
     def next_block():
         for n in ORDER:
-            run = [pos for pos in range(XS) if (n, pos) in left and a_need(pos) <= have]
-            if run and x_need(n) <= have:
-                stop = run[0] + 1
-                while stop in run:
-                    stop += 1
-                return n, run[0], stop
+            run = [pos for pos in range(BLOCKS) if (n, pos) in left and a_need(pos) <= have]
+            if not run or not x_need(n) <= have:
+                continue
+            stop = run[0] + 1
+            while stop in run:
+                stop += 1
+            if run[0] < FINE and (run[0] % 2 or stop - run[0] < 2):
+                continue
+            if stop % 2 and stop <= FINE:
+                stop -= 1
+            return n, run[0], stop
         return None
 
     def finish_ready():
         for r in range(RHS):
-            for pos in range(XS):
+            for pos in range(BLOCKS):
                 if (r, pos) in arrived and (RHS + r, pos) in made and (r, pos) not in finished:
                     finished.add((r, pos))
                     steps.append(("fin", r, pos))
-                    for link in (("x-",), ("x+",), ("x+", "x-"))[pos - 1] if pos else ():
+                    for link in (("x-",), ("x+",), ("x+", "x-"))[pos // 2 - 1] if pos > 1 else ():
                         done[0] = max(done[0], take(link, now, OUT_US) + HOP_US)
 
     while heap or left:
@@ -189,13 +203,13 @@
             if name[0] != "P":
                 steps.append(("wait", name))
             got(name, now)
-            pump(now, LOOKAHEAD_US)
+            pump(now, 0.0)
         block = next_block()
         if block is not None:
             n, lo, hi = block
             left = [b for b in left if b[0] != n or not lo <= b[1] < hi]
-            spent = BLOCK_US * (hi - lo)
-            pump(now, LOOKAHEAD_US + spent)
+            spent = BLOCK_US * (hi - lo) + BLOCK0_US
+            pump(now, spent)
             steps.append(("mm", n, lo, hi))
             now += spent
             made |= set((n, pos) for pos in range(lo, hi))
@@ -207,8 +221,8 @@
             finish_ready()
         elif heap:
             now = max(now, heap[0][0])
-        pump(now, LOOKAHEAD_US)
-    assert not any(pools.values()) and len(finished) == RHS * XS
+        pump(now, 0.0)
+    assert not any(pools.values()) and len(finished) == RHS * BLOCKS
     return steps, max(now, done[0])
 
 
@@ -261,7 +275,7 @@
 
         def a_slot(name):
             _, dx, dp, half, piece = name
-            return a_all.at[dp, pl.ds(POS[dx] * rows + half * hrows + piece * unit, unit), :]
+            return a_all.at[pl.ds(POS[dx] * rows + half * hrows + piece * unit, unit), pl.ds(dp * kcols, kcols)]
 
         def x_index(name):
             return name[1] * (depth_size + 1) + (depth_size if name == ("XH", name[1], 1) else mid if name[0] == "XH" else name[2])
@@ -291,7 +305,7 @@
         def columns(block):
             return pl.ds(pl.multiple_of(block * sub, sub), sub)
 
-        own_a = pltpu.make_async_copy(w_ref, a_all.at[0, pl.ds(0, rows), :], l_sem.at[1])
+        own_a = pltpu.make_async_copy(w_ref, a_all.at[pl.ds(0, rows), pl.ds(0, kcols)], l_sem.at[1])
 
         def exchange_x(r):
             s = lax.rem(xpos + x_col, 2)
@@ -310,36 +324,36 @@
                     remote(src, dst, ssem, rsem, at(hops, x_col))
 
         def matmul(n, lo, hi):
-            kstep = min(2048, kcols)
-            per = kcols // kstep
+            kstep = kcols if hi - lo <= 4 else kcols // 2
 
             def body(idx, carry):
-                dp = idx // per
-                k0 = pl.multiple_of(lax.rem(idx, per) * kstep, kstep)
-                lhs = a_all[dp, pl.ds(lo * rows, (hi - lo) * rows), pl.ds(k0, kstep)]
-                rhs = x_all[n, dp, pl.ds(k0, kstep), :]
-                part = jnp.dot(lhs, rhs, preferred_element_type=jnp.float32)
-                acc[n, pl.ds(lo, hi - lo)] += part.reshape(hi - lo, rows, sub)
+                k0 = pl.multiple_of(idx * kstep, kstep)
+                lhs = a_all[pl.ds(lo * hrows, (hi - lo) * hrows), pl.ds(k0, kstep)]
+                rhs = x_all[n, idx // (kcols // kstep), pl.ds(pl.multiple_of(lax.rem(k0, kcols), kstep), kstep), :]
+                prod = jnp.dot(lhs, rhs, preferred_element_type=jnp.float32)
+                acc[n, pl.ds(lo, hi - lo)] += prod.reshape(hi - lo, hrows, sub)
                 return carry
 
-            lax.fori_loop(0, 2 * per, body, 0)
+            lax.fori_loop(0, 2 * kcols // kstep, body, 0)
 
         def exchange_acc(n, lo, hi):
             span = pl.ds(lo, hi - lo)
-            remote(acc.at[n, span], peer_acc.at[n, span], e_ssem.at[n * XS + lo], e_rsem.at[n * XS + lo], links["yp"])
+            remote(acc.at[n, span], peer_acc.at[n, span], e_ssem.at[n * BLOCKS + lo], e_rsem.at[n * BLOCKS + lo], links["yp"])
 
         local = []
 
         def finish(r, pos):
-            dx = next(d for d in POS if POS[d] == pos)
+            dx = next(d for d in POS if POS[d] == pos // 2)
+            half = pos % 2
             y_buf[r, pos] = (acc[RHS + r, pos] + peer_acc[r, pos]).astype(y_buf.dtype)
-            src, dst = y_buf.at[r, pos], o_ref.at[r, :, columns(xpos)]
+            src, dst = y_buf.at[r, pos], o_ref.at[r, pl.ds(half * hrows, hrows), columns(xpos)]
+            sem = (r * XS + dx) * 2 + half
             if dx == 0:
-                copy = pltpu.make_async_copy(src, dst, y_ssem.at[r * XS])
+                copy = pltpu.make_async_copy(src, dst, y_ssem.at[sem])
                 copy.start()
                 local.append(copy)
             else:
-                remote(src, dst, y_ssem.at[r * XS + dx], y_rsem.at[r * XS + dx], at(XS - dx, col))
+                remote(src, dst, y_ssem.at[sem], y_rsem.at[sem], at(XS - dx, col))
 
         waited = set()
         for step in steps:
@@ -388,13 +402,15 @@
                 exchange_acc(*step[1:])
             elif step[0] == "peer":
                 _, n, lo, hi = step
-                landed(peer_acc.at[n, pl.ds(lo, hi - lo)], e_rsem.at[n * XS + lo])
+                landed(peer_acc.at[n, pl.ds(lo, hi - lo)], e_rsem.at[n * BLOCKS + lo])
             else:
                 finish(step[1], step[2])
 
         for r in range(RHS):
             for dx in range(1, XS):
-                landed(o_ref.at[r, :, columns(lax.rem(xpos + dx, XS))], y_rsem.at[r * XS + dx])
+                for half in range(2):
+                    slot = o_ref.at[r, pl.ds(half * hrows, hrows), columns(lax.rem(xpos + dx, XS))]
+                    landed(slot, y_rsem.at[(r * XS + dx) * 2 + half])
 
             @pl.when(cross == 1)
             def _():
@@ -419,13 +435,13 @@
             in_specs=[pl.BlockSpec(memory_space=pl.ANY)] * 2,
             out_specs=pl.BlockSpec(memory_space=pl.ANY),
             scratch_shapes=[
-                pltpu.VMEM((2, XS * rows, kcols), jnp.bfloat16),
+                pltpu.VMEM((XS * rows, 2 * kcols), jnp.bfloat16),
                 pltpu.VMEM((CHUNKS, 2, kcols, sub), jnp.bfloat16),
-                pltpu.VMEM((CHUNKS, XS, rows, sub), jnp.float32),
-                pltpu.VMEM((RHS, XS, rows, sub), jnp.float32),
-                pltpu.VMEM((RHS, XS, rows, sub), jnp.bfloat16),
+                pltpu.VMEM((CHUNKS, BLOCKS, rows // 2, sub), jnp.float32),
+                pltpu.VMEM((RHS, BLOCKS, rows // 2, sub), jnp.float32),
+                pltpu.VMEM((RHS, BLOCKS, rows // 2, sub), jnp.bfloat16),
                 *sems(32), *sems(CHUNKS * (depth_size + 1)), *sems(CHUNKS * depth_size),
-                dma((RHS * XS,)), dma((CHUNKS * 2,)), *sems(RHS * XS), *sems(RHS * XS), dma((2,)),
+                dma((RHS * XS,)), dma((CHUNKS * 2,)), *sems(RHS * BLOCKS), *sems(RHS * BLOCKS), dma((2,)),
             ],
             compiler_params=pltpu.CompilerParams(collective_id=0, has_side_effects=True, vmem_limit_bytes=67043328),
             cost_estimate=pl.CostEstimate(flops=2 * XS * rows * 2 * kcols * CHUNKS * sub, bytes_accessed=0, transcendentals=0),

time: 166 us -> 165 us (level)
  no operation moved by 1% of the time
where the time goes in v5:
time: 165 us
  Pallas kernels  162 us (98%)
  local copies, waits for them, and re-layouts  2.67 us (2%)
    pallas_call x1, Pallas kernels, local_product(): pl.pallas_call(kernel, out_shape=jax.ShapeDtypeStruct(x_local.shape, jnp....  162 us

profile of v5, /device:TPU:2, one launch (start us, length us, event | category | flops | bytes accessed | tf_op | source)
XLA Modules:
  0.0 164.6 jit_solution(11234827426978121014)
XLA Ops:
  0.0 161.9 %gather_matmul.1 = bf16[3,256,1024]{2,1,0:T(8,128)(2,1)} custom-call(bf16[256,4096]{1,0:T(8,128)(2,1)} %w_ref.1, bf16[3,256,1024]{2,1,0:T(8,128)(2,1)} %x_ref.1), custom_call_target="tpu_custom_call" | custom-call | flops 25769803776 | tf_op jit(solution)/shard_map/gather_matmul/pallas_call | solution.py:432
  161.9 2.7 %copy.4 = bf16[3,256,1024]{2,1,0:T(8,128)(2,1)} copy(bf16[3,256,1024]{2,1,0:T(8,128)(2,1)} %gather_matmul.1) | data formatting | bytes 3145728

commit v6 on v5

--- a/solution.py
+++ b/solution.py
@@ -14,24 +14,24 @@
 CHUNKS = 2 * RHS
 ORDER = (0, 1, 2, 3, 4, 5)
 BLOCKS = 2 * XS
-FINE = 8
+FINE = 6
 POS = {0: 0, 1: 1, 3: 2, 2: 3}
-READY = ((0,), (1,), (2,), (3,))
+READY = ((0,), (1, 3), (2,))
 
 A_UNIT_US = 11.3
 X_UNIT_US = 5.65
 T_X_US = 5.65
 T_Y_US = 11.3
-HOLD_US = (0.0, 0.0, 0.0, 9, 55, 66)
-A2A_AT_US = (0.0, 0.0, 24.4)
+HOLD_US = (0.0, 0.0, 0.0, 0.0, 37, 98)
+A2A_AT_US = (0.0, 4.6, 5.2)
 OUT_US = 1.41
 D2D_US = 1.5
 XCH_US = 2.83
-HOP_US = 2.5
-AHEAD_A_US = 2.4
-AHEAD_X_US = 2.5
-A_WEIGHTS = (1.3, 0.06, 0.78, -0.71)
-X_WEIGHTS = (0.4, 0.33)
+HOP_US = 2.8
+AHEAD_A_US = 1.1
+AHEAD_X_US = 2.7
+A_WEIGHTS = (0.96, 0.31, 0.16, -0.76)
+X_WEIGHTS = (0.57, 0.04)
 BLOCK_US = 0.55
 BLOCK0_US = 0.4
 LATE_US = 0.0

time: 165 us -> 164 us (level)
  no operation moved by 1% of the time
where the time goes in v6:
time: 164 us
  Pallas kernels  161 us (98%)
  local copies, waits for them, and re-layouts  2.67 us (2%)
    pallas_call x1, Pallas kernels, local_product(): pl.pallas_call(kernel, out_shape=jax.ShapeDtypeStruct(x_local.shape, jnp....  161 us

profile of v6, /device:TPU:2, one launch (start us, length us, event | category | flops | bytes accessed | tf_op | source)
XLA Modules:
  0.0 164.0 jit_solution(15382383947868951720)
XLA Ops:
  0.0 161.3 %gather_matmul.1 = bf16[3,256,1024]{2,1,0:T(8,128)(2,1)} custom-call(bf16[256,4096]{1,0:T(8,128)(2,1)} %w_ref.1, bf16[3,256,1024]{2,1,0:T(8,128)(2,1)} %x_ref.1), custom_call_target="tpu_custom_call" | custom-call | flops 25769803776 | tf_op jit(solution)/shard_map/gather_matmul/pallas_call | solution.py:432
  161.3 2.7 %copy.4 = bf16[3,256,1024]{2,1,0:T(8,128)(2,1)} copy(bf16[3,256,1024]{2,1,0:T(8,128)(2,1)} %gather_matmul.1) | data formatting | bytes 3145728
